TPU v7x, 128 devices: a whole 4x4x4 slice. The times are simulated.
128 devices in a mesh: atom: 32 (over x, z, core), energy: 4 (over y).
Axes of the slice: x: 4, y: 4, z: 4, core: 2. Of those that a mesh axis runs over, the one named last changes fastest.
Arguments:
- t_matrix: float32 [4, 256, 16, 16], P('energy', 'atom'), may hold values from -1.5 to 1.5
- structure: bfloat16 [4, 256, 1024, 1024], P('energy', 'atom'), may hold values from -0.125 to 0.125
- radial: bfloat16 [4, 256, 16, 1024], P('energy', 'atom'), may hold values from -3 to 3
- weights: float32 [4], P('energy'), may hold values from 0.1 to 1
- neighbours: int32 [256, 64], P('atom'), may hold values from 0 to 255, as said below
- live: int32 [256, 64], P('atom'), may hold values from 0 to 1, as said below
Outputs:
- density: float32 [256, 1024], P('atom', 'energy')
Inputs may be any that keep to these rules, and one draw needn't show every extreme that they name: `neighbours`: slot 0 of atom i holds i itself. Atom i lies at index i // 8 of the atom axis, and every neighbour of it lies at an index that differs from that one by at most 3 around the axis, which closes into a loop; both extremes occur in every draw. An atom may appear in several slots of one zone. `live`: each row is 1 on its first slots and 0 after; slot 0 is always 1, at least 16 slots are 1, and some atom has all 64 slots 1.
All inputs are finite; a program needn't handle non-finite values.
Results may differ from a plain program's by a relative error of at most 0.0043.
Values sent between devices are 32-bit elements; how exact they have to be, the bound alone decides.
A program may use at most 128 MiB of HBM per device.

v0:
```python
import functools

import jax
import jax.numpy as jnp
from jax import lax
from jax.experimental import pallas as pl
from jax.experimental.pallas import tpu as pltpu
from jax.sharding import PartitionSpec as P

MESH = pl.DeviceIdType.MESH
F32 = jnp.float32
BF16 = jnp.bfloat16

SPAN = 3
PLACES = 2 * SPAN + 1
SWEEPS = 4
LM = 16
NB = 64
A_DEV = 8
LANES = 128
SIZE = NB * LM
TILE = 256


def iota(shape, dim):
    return lax.broadcasted_iota(jnp.int32, shape, dim)


def ones_where(cond):
    return jnp.where(cond, 1.0, 0.0).astype(F32)


def kernel(
    n_atom, n_energy,
    t_ref, rad_ref, w_ref, nbr_ref, live_ref, s_hbm, out_ref,
    s_buf, st_buf, q_buf, bd_buf, table, t_self, t_land, first_buf, img_buf, spread_buf, tbx_buf, t_tiled,
    g_send, g_land, p_send, p_land, slot_of,
    s_sem, t_send_sem, t_recv_sem, g_send_sem, g_recv_sem, p_send_sem, p_recv_sem,
):
    me = lax.axis_index("atom")
    mine = lax.axis_index("energy")

    def atom_at(by):
        return lax.rem(me + by + n_atom, n_atom)

    def energy_at(by):
        return lax.rem(mine + by, n_energy)

    others = [place for place in range(PLACES) if place != SPAN]

    def s_copy(a):
        return pltpu.make_async_copy(s_hbm.at[a], s_buf.at[a], s_sem.at[a])

    for a in range(A_DEV):
        s_copy(a).start()

    barrier = pltpu.get_barrier_semaphore()
    for place in others:
        pl.semaphore_signal(barrier, inc=1, device_id={"atom": atom_at(place - SPAN)}, device_id_type=MESH)
    for by in range(1, n_energy):
        pl.semaphore_signal(barrier, inc=1, device_id={"energy": energy_at(by)}, device_id_type=MESH)

    t_rows = t_ref[...]
    t_wide = jnp.concatenate([t_rows, jnp.zeros((A_DEV * LM, LANES - LM), F32)], axis=1)
    t_turned = t_wide.T[0:LM, :]
    t_self[...] = t_turned
    lane16 = iota((LM, LANES), 1)
    for a in range(A_DEV):
        moved = t_turned if a == 0 else pltpu.roll(t_turned, LANES - a * LM, 1)
        first_buf[a] = jnp.where(lane16 < LM, moved, 0.0)

    pl.semaphore_wait(barrier, len(others) + n_energy - 1)

    def t_copy(place):
        return pltpu.make_async_remote_copy(
            src_ref=t_self, dst_ref=t_land.at[2 * SPAN - place],
            send_sem=t_send_sem.at[place], recv_sem=t_recv_sem.at[2 * SPAN - place],
            device_id={"atom": atom_at(place - SPAN)}, device_id_type=MESH,
        )

    for place in others:
        t_copy(place).start()

    lane = iota((LANES, LANES), 1)
    row = iota((LANES, LANES), 0)
    t_b = t_rows.astype(BF16)
    expand = ones_where(iota((LM, LANES), 1) // A_DEV == iota((LM, LANES), 0)).astype(BF16)
    tbx = jnp.dot(t_b, expand, preferred_element_type=F32)
    tbx = jnp.where(lane % A_DEV == row // LM, tbx, 0.0).astype(BF16)
    tbx_buf[:, 0:LANES] = tbx
    tbx_buf[:, LANES:] = tbx
    tiled = t_wide
    for by in (16, 32, 64):
        tiled = tiled + pltpu.roll(tiled, by, 1)
    t_tiled[...] = tiled
    for a in range(A_DEV):
        spread_buf[:, a * LANES:(a + 1) * LANES] = ones_where(
            (row // LM == a) & (row % LM == lane % LM)
        ).astype(BF16)

    where_to = lane16 - A_DEV * (iota((LM, LANES), 0) % 2)

    def hot(step, carry):
        a = step // (NB // 8)
        for k in range(8):
            s = (step % (NB // 8)) * 8 + k
            nbr = nbr_ref[a, s]
            alive = live_ref[a, s]
            place = lax.rem(nbr // A_DEV - me + SPAN + n_atom, n_atom)
            inner = lax.rem(nbr, A_DEV)
            base = alive * (place * LM + inner + 1) - 1
            slot_of[a, s] = alive * (place * A_DEV + inner - PLACES * A_DEV) + PLACES * A_DEV
            q_buf[a, pl.ds(pl.multiple_of(s * LM, LM), LM), :] = jnp.where(
                (where_to == base) & (base >= 0), 1.0, 0.0
            ).astype(BF16)
        return carry

    lax.fori_loop(0, A_DEV * NB // 8, hot, 0)

    def turn(a, carry):
        s_copy(a).wait()
        for bi in range(SIZE // TILE):
            for bj in range(SIZE // TILE):
                st_buf[a, bj * TILE:(bj + 1) * TILE, bi * TILE:(bi + 1) * TILE] = s_buf[
                    a, bi * TILE:(bi + 1) * TILE, bj * TILE:(bj + 1) * TILE
                ].T
        img_buf[a] = jnp.dot(
            first_buf[a].astype(BF16), st_buf[a, 0:LANES, :], preferred_element_type=F32
        ).astype(BF16)
        return carry

    lax.fori_loop(0, A_DEV, turn, 0)

    t_land[SPAN] = t_self[...]
    for place in others:
        t_copy(place).wait_send()
        t_copy(2 * SPAN - place).wait_recv()
    landed = t_land[...].reshape(PLACES * LM, LANES).astype(BF16)
    wide = jnp.dot(landed, spread_buf[...], preferred_element_type=F32).astype(BF16)
    for place in range(PLACES):
        for a in range(A_DEV):
            table[place * A_DEV + a] = wide[place * LM:(place + 1) * LM, a * LANES:(a + 1) * LANES]
    table[PLACES * A_DEV] = jnp.zeros((LM, LANES), BF16)

    keep = [ones_where(lane16 // LM == r).astype(BF16) for r in range(8)]

    def zone_blocks(a):
        for g in range(4):
            for h in range(2):
                for r in range(8):
                    s = g * 16 + h * 8 + r
                    bd_buf[a, g, r * LM:(r + 1) * LM, h * LANES:(h + 1) * LANES] = (
                        table[slot_of[a, s]] * keep[r]
                    )

    def zone(a):
        image = img_buf[a]
        parts = []
        for g in range(4):
            pair = jnp.concatenate(
                [image[:, 2 * g * LANES:(2 * g + 1) * LANES], image[:, (2 * g + 1) * LANES:(2 * g + 2) * LANES]],
                axis=0,
            )
            both = jnp.dot(pair, bd_buf[a, g], preferred_element_type=F32)
            parts.append(both[0:LM, 0:LANES])
            parts.append(both[LM:2 * LM, LANES:])
        parts[0] = parts[0] + first_buf[a]
        return jnp.concatenate([part.astype(BF16) for part in parts], axis=1)

    def sweep(a, flat):
        img_buf[a] = jnp.dot(flat, st_buf[a], preferred_element_type=F32).astype(BF16)

    for a in range(A_DEV):
        zone_blocks(a)
    for step in range(SWEEPS - 1):
        for a in range(A_DEV):
            sweep(a, zone(a))

    total = jnp.zeros((LANES, LANES), F32)
    pick = [ones_where((lane16 % LM) // 2 == h).astype(BF16) for h in range(8)]
    for a in range(A_DEV):
        image = img_buf[a]
        rows = jnp.concatenate([image * jnp.concatenate([pick[h]] * 8, axis=1) for h in range(8)], axis=0)
        total = total + jnp.dot(rows, q_buf[a], preferred_element_type=F32)
    g_send[...] = total.T

    def g_copy(place):
        return pltpu.make_async_remote_copy(
            src_ref=g_send.at[pl.ds(place * LM, LM)], dst_ref=g_land.at[2 * SPAN - place],
            send_sem=g_send_sem.at[place], recv_sem=g_recv_sem.at[2 * SPAN - place],
            device_id={"atom": atom_at(place - SPAN)}, device_id_type=MESH,
        )

    for place in others:
        g_copy(place).start()
    owned = g_send[SPAN * LM:(SPAN + 1) * LM, :]
    for place in others:
        g_copy(2 * SPAN - place).wait_recv()
        owned = owned + g_land[place]

    high = owned.astype(BF16)
    low = (owned - high.astype(F32)).astype(BF16)
    apart = ones_where(row // LM == lane // LM).astype(BF16)
    stacked = jnp.concatenate(
        [jnp.concatenate([high] * 8, axis=0) * apart, jnp.concatenate([low] * 8, axis=0) * apart], axis=0
    )
    received = jnp.dot(tbx_buf[...], stacked, preferred_element_type=F32)
    for by in (16, 32, 64):
        received = received + pltpu.roll(received, by, 1)
    received = received + t_tiled[...]
    received_b = received.astype(BF16) * apart
    radial = rad_ref[...]
    turned = jnp.dot(received_b, radial, preferred_element_type=F32)
    product = radial.astype(F32) * turned
    partial = product.reshape(A_DEV, LM, product.shape[1]).sum(axis=1) * w_ref[0]
    chunk = product.shape[1] // n_energy
    for e in range(n_energy):
        p_send[e] = partial[:, e * chunk:(e + 1) * chunk]

    def p_copy(by):
        return pltpu.make_async_remote_copy(
            src_ref=p_send.at[energy_at(by)], dst_ref=p_land.at[by - 1],
            send_sem=p_send_sem.at[by - 1], recv_sem=p_recv_sem.at[by - 1],
            device_id={"energy": energy_at(by)}, device_id_type=MESH,
        )

    for by in range(1, n_energy):
        p_copy(by).start()
    density = p_send[mine]
    for by in range(1, n_energy):
        p_copy(by).wait_recv()
        density = density + p_land[by - 1]
    out_ref[...] = density
    for place in others:
        g_copy(place).wait_send()
    for by in range(1, n_energy):
        p_copy(by).wait_send()


def shards(n_atom, n_energy, t_matrix, structure, radial, weights, neighbours, live):
    r = radial.shape[-1]
    vmem = pl.BlockSpec(memory_space=pltpu.VMEM)
    smem = pl.BlockSpec(memory_space=pltpu.SMEM)
    return pl.pallas_call(
        functools.partial(kernel, n_atom, n_energy),
        out_shape=jax.ShapeDtypeStruct((A_DEV, r // n_energy), F32),
        in_specs=[vmem, vmem, smem, smem, smem, pl.BlockSpec(memory_space=pl.ANY)],
        out_specs=vmem,
        scratch_shapes=[
            pltpu.VMEM((A_DEV, SIZE, SIZE), BF16),
            pltpu.VMEM((A_DEV, SIZE, SIZE), BF16),
            pltpu.VMEM((A_DEV, SIZE, LANES), BF16),
            pltpu.VMEM((A_DEV, 4, LANES, TILE), BF16),
            pltpu.VMEM((PLACES * A_DEV + 8, LM, LANES), BF16),
            pltpu.VMEM((LM, LANES), F32),
            pltpu.VMEM((PLACES, LM, LANES), F32),
            pltpu.VMEM((A_DEV, LM, LANES), F32),
            pltpu.VMEM((A_DEV, LM, SIZE), BF16),
            pltpu.VMEM((LANES, A_DEV * LANES), BF16),
            pltpu.VMEM((LANES, 2 * LANES), BF16),
            pltpu.VMEM((LANES, LANES), F32),
            pltpu.VMEM((LANES, LANES), F32),
            pltpu.VMEM((PLACES, LM, LANES), F32),
            pltpu.VMEM((n_energy, A_DEV, r // n_energy), F32),
            pltpu.VMEM((n_energy - 1, A_DEV, r // n_energy), F32),
            pltpu.SMEM((A_DEV, NB), jnp.int32),
            pltpu.SemaphoreType.DMA((A_DEV,)),
            pltpu.SemaphoreType.DMA((PLACES,)),
            pltpu.SemaphoreType.DMA((PLACES,)),
            pltpu.SemaphoreType.DMA((PLACES,)),
            pltpu.SemaphoreType.DMA((PLACES,)),
            pltpu.SemaphoreType.DMA((n_energy - 1,)),
            pltpu.SemaphoreType.DMA((n_energy - 1,)),
        ],
        compiler_params=pltpu.CompilerParams(
            collective_id=0, has_side_effects=True, vmem_limit_bytes=60 * 1024 * 1024
        ),
    )(
        t_matrix.reshape(A_DEV * LM, LM),
        radial.reshape(A_DEV * LM, r),
        weights,
        neighbours,
        live,
        structure.reshape(A_DEV, SIZE, SIZE),
    )


def solution(mesh):
    in_specs = (
        P("energy", "atom", None, None),
        P("energy", "atom", None, None),
        P("energy", "atom", None, None),
        P("energy"),
        P("atom", None),
        P("atom", None),
    )
    body = functools.partial(shards, mesh.shape["atom"], mesh.shape["energy"])
    return jax.shard_map(body, mesh=mesh, in_specs=in_specs, out_specs=P("atom", "energy"), check_vma=False)
```

profile of v0, /device:TPU:1, one launch (start us, length us, event | category | flops | bytes accessed | tf_op | source)
XLA Modules:
  0.0 42.7 jit_solution(13283999538454570425)
XLA Ops:
  0.7 40.7 %shard_map.64 = f32[8,256]{1,0:T(8,128)} custom-call(f32[128,16]{1,0:T(8,128)} %bitcast.5, bf16[128,1024]{1,0:T(8,128)(2,1)} %bitcast.4, f32[1]{0:T(128)S(6)} %copy.8.w_ref, s32[8,64]{1,0:T(8,128)} %nbr_ref.1, s32[8,64]{1,0:T(8,128)} %live_ref.1, bf16[8,1024,1024]{2,1,0:T(8,128)(2,1)} %bitcast.3), custom_call_target="tpu_custom_call" | custom-call | tf_op jit(solution)/shard_map/pallas_call | solution.py:244
  41.4 1.3 %copy.9 = f32[8,256]{1,0:T(8,128)} copy(f32[8,256]{1,0:T(8,128)} %shard_map.64) | data formatting | bytes 16384
where the time goes:
time: 42.9 us; the launch traced here: 42.7 us
  Pallas kernels  40.7 us (95%)
  local copies, waits for them, and re-layouts  1.3 us (3%)
  between operations  0.66 us (2%)
    pallas_call x1, Pallas kernels, shards(): pl.pallas_call(functools.partial(kernel, n_atom, n_energy), out_shape=jax...  40.7 us
    unnamed x1, local copies, waits for them, and re-layouts  1.3 us

commit v1 on v0

--- a/solution.py
+++ b/solution.py
@@ -20,6 +20,7 @@
 LANES = 128
 SIZE = NB * LM
 TILE = 256
+EARLY = 3
 
 
 def iota(shape, dim):
@@ -32,10 +33,10 @@
 
 def kernel(
     n_atom, n_energy,
-    t_ref, rad_ref, w_ref, nbr_ref, live_ref, s_hbm, out_ref,
-    s_buf, st_buf, q_buf, bd_buf, table, t_self, t_land, first_buf, img_buf, spread_buf, tbx_buf, t_tiled,
+    t_hbm, rad_hbm, w_ref, nbr_hbm, live_hbm, s_hbm, out_ref,
+    t_ref, rad_ref, nbr_ref, live_ref, slot_vec, pattern, s_buf, st_buf, q_buf, bd_buf, table, t_self, t_land, first_buf, img_buf, spread_buf, tbx_buf, t_tiled,
     g_send, g_land, p_send, p_land, slot_of,
-    s_sem, t_send_sem, t_recv_sem, g_send_sem, g_recv_sem, p_send_sem, p_recv_sem,
+    in_sem, s_sem, t_send_sem, t_recv_sem, g_send_sem, g_recv_sem, p_send_sem, p_recv_sem,
 ):
     me = lax.axis_index("atom")
     mine = lax.axis_index("energy")
@@ -48,11 +49,13 @@
 
     others = [place for place in range(PLACES) if place != SPAN]
 
-    def s_copy(a):
-        return pltpu.make_async_copy(s_hbm.at[a], s_buf.at[a], s_sem.at[a])
-
-    for a in range(A_DEV):
-        s_copy(a).start()
+    t_in = pltpu.make_async_copy(t_hbm, t_ref, in_sem.at[0])
+    nbr_in = pltpu.make_async_copy(nbr_hbm, nbr_ref, in_sem.at[1])
+    live_in = pltpu.make_async_copy(live_hbm, live_ref, in_sem.at[2])
+    rad_in = pltpu.make_async_copy(rad_hbm, rad_ref, in_sem.at[3])
+    t_in.start()
+    nbr_in.start()
+    live_in.start()
 
     barrier = pltpu.get_barrier_semaphore()
     for place in others:
@@ -60,6 +63,14 @@
     for by in range(1, n_energy):
         pl.semaphore_signal(barrier, inc=1, device_id={"energy": energy_at(by)}, device_id_type=MESH)
 
+    def s_copy(a):
+        return pltpu.make_async_copy(s_hbm.at[a], s_buf.at[a], s_sem.at[a])
+
+    for a in range(A_DEV):
+        s_copy(a).start()
+    rad_in.start()
+
+    t_in.wait()
     t_rows = t_ref[...]
     t_wide = jnp.concatenate([t_rows, jnp.zeros((A_DEV * LM, LANES - LM), F32)], axis=1)
     t_turned = t_wide.T[0:LM, :]
@@ -69,6 +80,27 @@
         moved = t_turned if a == 0 else pltpu.roll(t_turned, LANES - a * LM, 1)
         first_buf[a] = jnp.where(lane16 < LM, moved, 0.0)
 
+    nbr_in.wait()
+    live_in.wait()
+    nbr = nbr_ref[...]
+    place = lax.rem(nbr // A_DEV - me + SPAN + n_atom, n_atom)
+    slot_vec[...] = jnp.where(live_ref[...] > 0, place * A_DEV + lax.rem(nbr, A_DEV), PLACES * A_DEV)
+    slot_out = pltpu.make_async_copy(slot_vec, slot_of, in_sem.at[4])
+    slot_out.start()
+
+    def turn(a, carry):
+        s_copy(a).wait()
+        for bi in range(SIZE // TILE):
+            for bj in range(SIZE // TILE):
+                st_buf[a, bj * TILE:(bj + 1) * TILE, bi * TILE:(bi + 1) * TILE] = s_buf[
+                    a, bi * TILE:(bi + 1) * TILE, bj * TILE:(bj + 1) * TILE
+                ].T
+        img_buf[a] = jnp.dot(
+            first_buf[a].astype(BF16), st_buf[a, 0:LANES, :], preferred_element_type=F32
+        ).astype(BF16)
+        return carry
+
+    lax.fori_loop(0, EARLY, turn, 0)
     pl.semaphore_wait(barrier, len(others) + n_energy - 1)
 
     def t_copy(place):
@@ -98,38 +130,21 @@
             (row // LM == a) & (row % LM == lane % LM)
         ).astype(BF16)
 
+    lax.fori_loop(EARLY, A_DEV, turn, 0)
+
     where_to = lane16 - A_DEV * (iota((LM, LANES), 0) % 2)
-
-    def hot(step, carry):
-        a = step // (NB // 8)
-        for k in range(8):
-            s = (step % (NB // 8)) * 8 + k
-            nbr = nbr_ref[a, s]
-            alive = live_ref[a, s]
-            place = lax.rem(nbr // A_DEV - me + SPAN + n_atom, n_atom)
-            inner = lax.rem(nbr, A_DEV)
-            base = alive * (place * LM + inner + 1) - 1
-            slot_of[a, s] = alive * (place * A_DEV + inner - PLACES * A_DEV) + PLACES * A_DEV
-            q_buf[a, pl.ds(pl.multiple_of(s * LM, LM), LM), :] = jnp.where(
-                (where_to == base) & (base >= 0), 1.0, 0.0
-            ).astype(BF16)
+    for place in range(PLACES):
+        for a in range(A_DEV):
+            pattern[place * A_DEV + a] = ones_where(where_to == place * LM + a).astype(BF16)
+    pattern[PLACES * A_DEV] = jnp.zeros((LM, LANES), BF16)
+    slot_out.wait()
+
+    def hot(a, carry):
+        for s in range(NB):
+            q_buf[a, s * LM:(s + 1) * LM, :] = pattern[slot_of[a, s]]
         return carry
 
-    lax.fori_loop(0, A_DEV * NB // 8, hot, 0)
-
-    def turn(a, carry):
-        s_copy(a).wait()
-        for bi in range(SIZE // TILE):
-            for bj in range(SIZE // TILE):
-                st_buf[a, bj * TILE:(bj + 1) * TILE, bi * TILE:(bi + 1) * TILE] = s_buf[
-                    a, bi * TILE:(bi + 1) * TILE, bj * TILE:(bj + 1) * TILE
-                ].T
-        img_buf[a] = jnp.dot(
-            first_buf[a].astype(BF16), st_buf[a, 0:LANES, :], preferred_element_type=F32
-        ).astype(BF16)
-        return carry
-
-    lax.fori_loop(0, A_DEV, turn, 0)
+    lax.fori_loop(0, A_DEV, hot, 0)
 
     t_land[SPAN] = t_self[...]
     for place in others:
@@ -170,10 +185,10 @@
     def sweep(a, flat):
         img_buf[a] = jnp.dot(flat, st_buf[a], preferred_element_type=F32).astype(BF16)
 
-    for a in range(A_DEV):
-        zone_blocks(a)
     for step in range(SWEEPS - 1):
         for a in range(A_DEV):
+            if step == 0:
+                zone_blocks(a)
             sweep(a, zone(a))
 
     total = jnp.zeros((LANES, LANES), F32)
@@ -209,6 +224,7 @@
         received = received + pltpu.roll(received, by, 1)
     received = received + t_tiled[...]
     received_b = received.astype(BF16) * apart
+    rad_in.wait()
     radial = rad_ref[...]
     turned = jnp.dot(received_b, radial, preferred_element_type=F32)
     product = radial.astype(F32) * turned
@@ -241,12 +257,19 @@
     r = radial.shape[-1]
     vmem = pl.BlockSpec(memory_space=pltpu.VMEM)
     smem = pl.BlockSpec(memory_space=pltpu.SMEM)
+    hbm = pl.BlockSpec(memory_space=pl.ANY)
     return pl.pallas_call(
         functools.partial(kernel, n_atom, n_energy),
         out_shape=jax.ShapeDtypeStruct((A_DEV, r // n_energy), F32),
-        in_specs=[vmem, vmem, smem, smem, smem, pl.BlockSpec(memory_space=pl.ANY)],
+        in_specs=[hbm, hbm, smem, hbm, hbm, hbm],
         out_specs=vmem,
         scratch_shapes=[
+            pltpu.VMEM((A_DEV * LM, LM), F32),
+            pltpu.VMEM((A_DEV * LM, r), BF16),
+            pltpu.VMEM((A_DEV, NB), jnp.int32),
+            pltpu.VMEM((A_DEV, NB), jnp.int32),
+            pltpu.VMEM((A_DEV, NB), jnp.int32),
+            pltpu.VMEM((PLACES * A_DEV + 8, LM, LANES), BF16),
             pltpu.VMEM((A_DEV, SIZE, SIZE), BF16),
             pltpu.VMEM((A_DEV, SIZE, SIZE), BF16),
             pltpu.VMEM((A_DEV, SIZE, LANES), BF16),
@@ -264,6 +287,7 @@
             pltpu.VMEM((n_energy, A_DEV, r // n_energy), F32),
             pltpu.VMEM((n_energy - 1, A_DEV, r // n_energy), F32),
             pltpu.SMEM((A_DEV, NB), jnp.int32),
+            pltpu.SemaphoreType.DMA((5,)),
             pltpu.SemaphoreType.DMA((A_DEV,)),
             pltpu.SemaphoreType.DMA((PLACES,)),
             pltpu.SemaphoreType.DMA((PLACES,)),

time: 42.9 us -> 34.6 us (0.81)
  Pallas kernels: 40.7 us -> 32.5 us
    pallas_call x1, Pallas kernels: 40.7 us -> 32.5 us  [shards(): pl.pallas_call(functools.partial(kernel, n_atom, n_energy), out_shape=jax...]
where the time goes in v1:
time: 34.6 us; the launch traced here: 34.4 us
  Pallas kernels  32.5 us (94%)
  local copies, waits for them, and re-layouts  1.3 us (4%)
  between operations  0.66 us (2%)
    pallas_call x1, Pallas kernels, shards(): pl.pallas_call(functools.partial(kernel, n_atom, n_energy), out_shape=jax...  32.5 us
    unnamed x1, local copies, waits for them, and re-layouts  1.3 us

profile of v1, /device:TPU:1, one launch (start us, length us, event | category | flops | bytes accessed | tf_op | source)
XLA Modules:
  0.0 34.4 jit_solution(2124108141287962238)
XLA Ops:
  0.7 32.5 %shard_map.64 = f32[8,256]{1,0:T(8,128)} custom-call(f32[128,16]{1,0:T(8,128)} %bitcast.5, bf16[128,1024]{1,0:T(8,128)(2,1)} %bitcast.4, f32[1]{0:T(128)S(6)} %copy.8.w_ref, s32[8,64]{1,0:T(8,128)} %nbr_hbm.1, s32[8,64]{1,0:T(8,128)} %live_hbm.1, bf16[8,1024,1024]{2,1,0:T(8,128)(2,1)} %bitcast.3), custom_call_target="tpu_custom_call" | custom-call | tf_op jit(solution)/shard_map/pallas_call | solution.py:261
  33.1 1.3 %copy.9 = f32[8,256]{1,0:T(8,128)} copy(f32[8,256]{1,0:T(8,128)} %shard_map.64) | data formatting | bytes 16384

commit v2 on v1

--- a/solution.py
+++ b/solution.py
@@ -20,7 +20,7 @@
 LANES = 128
 SIZE = NB * LM
 TILE = 256
-EARLY = 3
+EARLY = 1
 
 
 def iota(shape, dim):
@@ -33,8 +33,8 @@
 
 def kernel(
     n_atom, n_energy,
-    t_hbm, rad_hbm, w_ref, nbr_hbm, live_hbm, s_hbm, out_ref,
-    t_ref, rad_ref, nbr_ref, live_ref, slot_vec, pattern, s_buf, st_buf, q_buf, bd_buf, table, t_self, t_land, first_buf, img_buf, spread_buf, tbx_buf, t_tiled,
+    t_hbm, rad_hbm, w_hbm, nbr_hbm, live_hbm, s_hbm, out_ref,
+    t_ref, rad_ref, w_ref, nbr_ref, live_ref, slot_vec, pattern, s_buf, st_buf, q_buf, bd_buf, table, t_self, t_land, first_buf, img_buf, spread_buf, tbx_buf, t_tiled,
     g_send, g_land, p_send, p_land, slot_of,
     in_sem, s_sem, t_send_sem, t_recv_sem, g_send_sem, g_recv_sem, p_send_sem, p_recv_sem,
 ):
@@ -53,6 +53,7 @@
     nbr_in = pltpu.make_async_copy(nbr_hbm, nbr_ref, in_sem.at[1])
     live_in = pltpu.make_async_copy(live_hbm, live_ref, in_sem.at[2])
     rad_in = pltpu.make_async_copy(rad_hbm, rad_ref, in_sem.at[3])
+    w_in = pltpu.make_async_copy(w_hbm, w_ref, in_sem.at[5])
     t_in.start()
     nbr_in.start()
     live_in.start()
@@ -69,6 +70,7 @@
     for a in range(A_DEV):
         s_copy(a).start()
     rad_in.start()
+    w_in.start()
 
     t_in.wait()
     t_rows = t_ref[...]
@@ -99,19 +101,6 @@
             first_buf[a].astype(BF16), st_buf[a, 0:LANES, :], preferred_element_type=F32
         ).astype(BF16)
         return carry
-
-    lax.fori_loop(0, EARLY, turn, 0)
-    pl.semaphore_wait(barrier, len(others) + n_energy - 1)
-
-    def t_copy(place):
-        return pltpu.make_async_remote_copy(
-            src_ref=t_self, dst_ref=t_land.at[2 * SPAN - place],
-            send_sem=t_send_sem.at[place], recv_sem=t_recv_sem.at[2 * SPAN - place],
-            device_id={"atom": atom_at(place - SPAN)}, device_id_type=MESH,
-        )
-
-    for place in others:
-        t_copy(place).start()
 
     lane = iota((LANES, LANES), 1)
     row = iota((LANES, LANES), 0)
@@ -130,7 +119,18 @@
             (row // LM == a) & (row % LM == lane % LM)
         ).astype(BF16)
 
-    lax.fori_loop(EARLY, A_DEV, turn, 0)
+    lax.fori_loop(0, EARLY, turn, 0)
+    pl.semaphore_wait(barrier, len(others) + n_energy - 1)
+
+    def t_copy(place):
+        return pltpu.make_async_remote_copy(
+            src_ref=t_self, dst_ref=t_land.at[2 * SPAN - place],
+            send_sem=t_send_sem.at[place], recv_sem=t_recv_sem.at[2 * SPAN - place],
+            device_id={"atom": atom_at(place - SPAN)}, device_id_type=MESH,
+        )
+
+    for place in others:
+        t_copy(place).start()
 
     where_to = lane16 - A_DEV * (iota((LM, LANES), 0) % 2)
     for place in range(PLACES):
@@ -145,6 +145,9 @@
         return carry
 
     lax.fori_loop(0, A_DEV, hot, 0)
+
+    lax.fori_loop(EARLY, A_DEV, turn, 0)
+
 
     t_land[SPAN] = t_self[...]
     for place in others:
@@ -185,18 +188,28 @@
     def sweep(a, flat):
         img_buf[a] = jnp.dot(flat, st_buf[a], preferred_element_type=F32).astype(BF16)
 
-    for step in range(SWEEPS - 1):
-        for a in range(A_DEV):
-            if step == 0:
-                zone_blocks(a)
-            sweep(a, zone(a))
-
-    total = jnp.zeros((LANES, LANES), F32)
     pick = [ones_where((lane16 % LM) // 2 == h).astype(BF16) for h in range(8)]
-    for a in range(A_DEV):
+
+    def zone_sum(a):
         image = img_buf[a]
         rows = jnp.concatenate([image * jnp.concatenate([pick[h]] * 8, axis=1) for h in range(8)], axis=0)
-        total = total + jnp.dot(rows, q_buf[a], preferred_element_type=F32)
+        return jnp.dot(rows, q_buf[a], preferred_element_type=F32)
+
+    order = [(step, a) for step in range(SWEEPS - 1) for a in range(A_DEV)]
+    zone_blocks(0)
+    flat = zone(0)
+    total = jnp.zeros((LANES, LANES), F32)
+    for n, (step, a) in enumerate(order):
+        ahead = None
+        if n + 1 < len(order):
+            if order[n + 1][0] == 0:
+                zone_blocks(order[n + 1][1])
+            ahead = zone(order[n + 1][1])
+        if step == SWEEPS - 2 and a > 0:
+            total = total + zone_sum(a - 1)
+        sweep(a, flat)
+        flat = ahead
+    total = total + zone_sum(A_DEV - 1)
     g_send[...] = total.T
 
     def g_copy(place):
@@ -225,6 +238,7 @@
     received = received + t_tiled[...]
     received_b = received.astype(BF16) * apart
     rad_in.wait()
+    w_in.wait()
     radial = rad_ref[...]
     turned = jnp.dot(received_b, radial, preferred_element_type=F32)
     product = radial.astype(F32) * turned
@@ -256,16 +270,16 @@
 def shards(n_atom, n_energy, t_matrix, structure, radial, weights, neighbours, live):
     r = radial.shape[-1]
     vmem = pl.BlockSpec(memory_space=pltpu.VMEM)
-    smem = pl.BlockSpec(memory_space=pltpu.SMEM)
     hbm = pl.BlockSpec(memory_space=pl.ANY)
     return pl.pallas_call(
         functools.partial(kernel, n_atom, n_energy),
-        out_shape=jax.ShapeDtypeStruct((A_DEV, r // n_energy), F32),
-        in_specs=[hbm, hbm, smem, hbm, hbm, hbm],
+        out_shape=pltpu.VMEM((A_DEV, r // n_energy), F32),
+        in_specs=[hbm] * 6,
         out_specs=vmem,
         scratch_shapes=[
             pltpu.VMEM((A_DEV * LM, LM), F32),
             pltpu.VMEM((A_DEV * LM, r), BF16),
+            pltpu.SMEM((1,), F32),
             pltpu.VMEM((A_DEV, NB), jnp.int32),
             pltpu.VMEM((A_DEV, NB), jnp.int32),
             pltpu.VMEM((A_DEV, NB), jnp.int32),
@@ -287,7 +301,7 @@
             pltpu.VMEM((n_energy, A_DEV, r // n_energy), F32),
             pltpu.VMEM((n_energy - 1, A_DEV, r // n_energy), F32),
             pltpu.SMEM((A_DEV, NB), jnp.int32),
-            pltpu.SemaphoreType.DMA((5,)),
+            pltpu.SemaphoreType.DMA((6,)),
             pltpu.SemaphoreType.DMA((A_DEV,)),
             pltpu.SemaphoreType.DMA((PLACES,)),
             pltpu.SemaphoreType.DMA((PLACES,)),

time: 34.6 us -> 31.8 us (0.919)
  Pallas kernels: 32.5 us -> 30.4 us
  local copies, waits for them, and re-layouts: 1.3 us -> 0.6 us
    pallas_call x1, Pallas kernels: 32.5 us -> 30.4 us  [shards(): pl.pallas_call(functools.partial(kernel, n_atom, n_energy), out_shape=plt...]
    unnamed x1, local copies, waits for them, and re-layouts: 1.3 us -> 0.6 us
where the time goes in v2:
time: 31.8 us; the launch traced here: 31.7 us
  Pallas kernels  30.4 us (96%)
  between operations  0.66 us (2%)
  local copies, waits for them, and re-layouts  0.6 us (2%)
    pallas_call x1, Pallas kernels, shards(): pl.pallas_call(functools.partial(kernel, n_atom, n_energy), out_shape=plt...  30.4 us

profile of v2, /device:TPU:1, one launch (start us, length us, event | category | flops | bytes accessed | tf_op | source)
XLA Modules:
  0.0 31.7 jit_solution(11404092987011656675)
XLA Ops:
  0.7 30.4 %shard_map.64 = f32[8,256]{1,0:T(8,128)S(1)} custom-call(f32[128,16]{1,0:T(8,128)} %bitcast.5, bf16[128,1024]{1,0:T(8,128)(2,1)} %bitcast.4, f32[1]{0:T(128)S(6)} %copy.9.w_hbm, s32[8,64]{1,0:T(8,128)} %nbr_hbm.1, s32[8,64]{1,0:T(8,128)} %live_hbm.1, bf16[8,1024,1024]{2,1,0:T(8,128)(2,1)} %bitcast.3), custom_call_target="tpu_custom_call" | custom-call | tf_op jit(solution)/shard_map/pallas_call | solution.py:274
  31.1 0.6 %copy.8 = f32[8,256]{1,0:T(8,128)} copy(f32[8,256]{1,0:T(8,128)S(1)} %shard_map.64) | data formatting | bytes 16384

commit v3 on v2

--- a/solution.py
+++ b/solution.py
@@ -20,7 +20,9 @@
 LANES = 128
 SIZE = NB * LM
 TILE = 256
-EARLY = 1
+EARLY = 0
+MIDDLE = 3
+ROW = 8
 
 
 def iota(shape, dim):
@@ -36,7 +38,7 @@
     t_hbm, rad_hbm, w_hbm, nbr_hbm, live_hbm, s_hbm, out_ref,
     t_ref, rad_ref, w_ref, nbr_ref, live_ref, slot_vec, pattern, s_buf, st_buf, q_buf, bd_buf, table, t_self, t_land, first_buf, img_buf, spread_buf, tbx_buf, t_tiled,
     g_send, g_land, p_send, p_land, slot_of,
-    in_sem, s_sem, t_send_sem, t_recv_sem, g_send_sem, g_recv_sem, p_send_sem, p_recv_sem,
+    same, fed, feed_sem, ready, in_sem, s_sem, t_send_sem, t_recv_sem, g_send_sem, g_recv_sem, p_send_sem, p_recv_sem,
 ):
     me = lax.axis_index("atom")
     mine = lax.axis_index("energy")
@@ -59,8 +61,16 @@
     live_in.start()
 
     barrier = pltpu.get_barrier_semaphore()
-    for place in others:
-        pl.semaphore_signal(barrier, inc=1, device_id={"atom": atom_at(place - SPAN)}, device_id_type=MESH)
+    spot = lax.rem(me, ROW)
+
+    def greet(by):
+        pl.semaphore_signal(barrier, inc=1, device_id={"atom": atom_at(by)}, device_id_type=MESH)
+
+    for d in range(1, SPAN + 1):
+        greet(-d)
+        pl.when(spot + d < ROW)(functools.partial(greet, d))
+        pl.when(spot < d)(functools.partial(greet, ROW - d))
+    greet(ROW)
     for by in range(1, n_energy):
         pl.semaphore_signal(barrier, inc=1, device_id={"energy": energy_at(by)}, device_id_type=MESH)
 
@@ -90,13 +100,20 @@
     slot_out = pltpu.make_async_copy(slot_vec, slot_of, in_sem.at[4])
     slot_out.start()
 
+    same[...] = ones_where(iota((TILE, TILE), 0) == iota((TILE, TILE), 1)).astype(BF16)
+
     def turn(a, carry):
         s_copy(a).wait()
         for bi in range(SIZE // TILE):
             for bj in range(SIZE // TILE):
-                st_buf[a, bj * TILE:(bj + 1) * TILE, bi * TILE:(bi + 1) * TILE] = s_buf[
-                    a, bi * TILE:(bi + 1) * TILE, bj * TILE:(bj + 1) * TILE
-                ].T
+                tile = s_buf[a, bi * TILE:(bi + 1) * TILE, bj * TILE:(bj + 1) * TILE]
+                if (bi * 4 + bj) % 3 == 1:
+                    tile = lax.dot_general(
+                        same[...], tile, (((1,), (1,)), ((), ())), preferred_element_type=F32
+                    ).astype(BF16)
+                else:
+                    tile = tile.T
+                st_buf[a, bj * TILE:(bj + 1) * TILE, bi * TILE:(bi + 1) * TILE] = tile
         img_buf[a] = jnp.dot(
             first_buf[a].astype(BF16), st_buf[a, 0:LANES, :], preferred_element_type=F32
         ).astype(BF16)
@@ -120,17 +137,34 @@
         ).astype(BF16)
 
     lax.fori_loop(0, EARLY, turn, 0)
-    pl.semaphore_wait(barrier, len(others) + n_energy - 1)
-
-    def t_copy(place):
+    greeted = SPAN + jnp.minimum(spot, SPAN) + jnp.maximum(spot + SPAN + 1 - ROW, 0) + 1 + n_energy - 1
+    pl.semaphore_wait(barrier, greeted)
+
+    def t_copy(src, by, place):
         return pltpu.make_async_remote_copy(
-            src_ref=t_self, dst_ref=t_land.at[2 * SPAN - place],
-            send_sem=t_send_sem.at[place], recv_sem=t_recv_sem.at[2 * SPAN - place],
-            device_id={"atom": atom_at(place - SPAN)}, device_id_type=MESH,
+            src_ref=src, dst_ref=t_land.at[place],
+            send_sem=t_send_sem.at[place], recv_sem=t_recv_sem.at[place],
+            device_id={"atom": atom_at(by)}, device_id_type=MESH,
         )
 
-    for place in others:
-        t_copy(place).start()
+    def feed():
+        return pltpu.make_async_remote_copy(
+            src_ref=t_self, dst_ref=fed, send_sem=feed_sem.at[0], recv_sem=feed_sem.at[1],
+            device_id={"atom": atom_at(-ROW)}, device_id_type=MESH,
+        )
+
+    def t_down(d):
+        t_copy(t_self, -d, SPAN + d).start()
+
+    def ask(d):
+        pl.semaphore_signal(ready.at[d - 1], inc=1, device_id={"atom": atom_at(d - ROW)}, device_id_type=MESH)
+
+    feed().start()
+    for d in range(1, SPAN + 1):
+        pl.when(spot + d >= ROW)(functools.partial(ask, d))
+    for d in range(1, SPAN + 1):
+        t_copy(t_self, d, SPAN - d).start()
+        pl.when(spot >= d)(functools.partial(t_down, d))
 
     where_to = lane16 - A_DEV * (iota((LM, LANES), 0) % 2)
     for place in range(PLACES):
@@ -146,13 +180,21 @@
 
     lax.fori_loop(0, A_DEV, hot, 0)
 
-    lax.fori_loop(EARLY, A_DEV, turn, 0)
+    lax.fori_loop(EARLY, MIDDLE, turn, 0)
+
+    def forward(d):
+        pl.semaphore_wait(ready.at[d - 1], 1)
+        t_copy(fed, ROW - d, SPAN + d).start()
+
+    pl.when(spot < SPAN)(lambda: feed().wait_recv())
+    for d in range(SPAN, 0, -1):
+        pl.when(spot < d)(functools.partial(forward, d))
+    lax.fori_loop(MIDDLE, A_DEV, turn, 0)
 
 
     t_land[SPAN] = t_self[...]
     for place in others:
-        t_copy(place).wait_send()
-        t_copy(2 * SPAN - place).wait_recv()
+        t_copy(t_self, place - SPAN, place).wait_recv()
     landed = t_land[...].reshape(PLACES * LM, LANES).astype(BF16)
     wide = jnp.dot(landed, spread_buf[...], preferred_element_type=F32).astype(BF16)
     for place in range(PLACES):
@@ -226,17 +268,19 @@
         g_copy(2 * SPAN - place).wait_recv()
         owned = owned + g_land[place]
 
-    high = owned.astype(BF16)
-    low = (owned - high.astype(F32)).astype(BF16)
     apart = ones_where(row // LM == lane // LM).astype(BF16)
-    stacked = jnp.concatenate(
-        [jnp.concatenate([high] * 8, axis=0) * apart, jnp.concatenate([low] * 8, axis=0) * apart], axis=0
-    )
-    received = jnp.dot(tbx_buf[...], stacked, preferred_element_type=F32)
-    for by in (16, 32, 64):
-        received = received + pltpu.roll(received, by, 1)
-    received = received + t_tiled[...]
-    received_b = received.astype(BF16) * apart
+    moved = [owned if d == 0 else pltpu.roll(owned, d * LM, 1) for d in range(8)]
+    blocks = []
+    for h in range(8):
+        block = moved[(8 - h) % 8]
+        for x in range(1, 8):
+            block = jnp.where(lane16 // LM == x, moved[(x - h) % 8], block)
+        blocks.append(block)
+    owned_rows = jnp.concatenate(blocks, axis=0)
+    high = owned_rows.astype(BF16)
+    low = (owned_rows - high.astype(F32)).astype(BF16)
+    received = jnp.dot(tbx_buf[...], jnp.concatenate([high, low], axis=0), preferred_element_type=F32)
+    received_b = (received + t_tiled[...]).astype(BF16) * apart
     rad_in.wait()
     w_in.wait()
     radial = rad_ref[...]
@@ -261,7 +305,10 @@
         p_copy(by).wait_recv()
         density = density + p_land[by - 1]
     out_ref[...] = density
+    pl.when(spot >= SPAN)(lambda: feed().wait_recv())
+    feed().wait_send()
     for place in others:
+        t_copy(t_self, place - SPAN, place).wait_send()
         g_copy(place).wait_send()
     for by in range(1, n_energy):
         p_copy(by).wait_send()
@@ -301,6 +348,10 @@
             pltpu.VMEM((n_energy, A_DEV, r // n_energy), F32),
             pltpu.VMEM((n_energy - 1, A_DEV, r // n_energy), F32),
             pltpu.SMEM((A_DEV, NB), jnp.int32),
+            pltpu.VMEM((TILE, TILE), BF16),
+            pltpu.VMEM((LM, LANES), F32),
+            pltpu.SemaphoreType.DMA((2,)),
+            pltpu.SemaphoreType.REGULAR((SPAN,)),
             pltpu.SemaphoreType.DMA((6,)),
             pltpu.SemaphoreType.DMA((A_DEV,)),
             pltpu.SemaphoreType.DMA((PLACES,)),

time: 31.8 us -> 30.8 us (0.969)
  Pallas kernels: 30.4 us -> 29.5 us
    pallas_call x1, Pallas kernels: 30.4 us -> 29.5 us  [shards(): pl.pallas_call(functools.partial(kernel, n_atom, n_energy), out_shape=plt...]
where the time goes in v3:
time: 30.8 us; the launch traced here: 30.7 us
  Pallas kernels  29.5 us (96%)
  between operations  0.66 us (2%)
  local copies, waits for them, and re-layouts  0.6 us (2%)
    pallas_call x1, Pallas kernels, shards(): pl.pallas_call(functools.partial(kernel, n_atom, n_energy), out_shape=plt...  29.5 us

profile of v3, /device:TPU:1, one launch (start us, length us, event | category | flops | bytes accessed | tf_op | source)
XLA Modules:
  0.0 30.7 jit_solution(17572128131617729771)
XLA Ops:
  0.7 29.5 %shard_map.64 = f32[8,256]{1,0:T(8,128)S(1)} custom-call(f32[128,16]{1,0:T(8,128)} %bitcast.5, bf16[128,1024]{1,0:T(8,128)(2,1)} %bitcast.4, f32[1]{0:T(128)S(6)} %copy.9.w_hbm, s32[8,64]{1,0:T(8,128)} %nbr_hbm.1, s32[8,64]{1,0:T(8,128)} %live_hbm.1, bf16[8,1024,1024]{2,1,0:T(8,128)(2,1)} %bitcast.3), custom_call_target="tpu_custom_call" | custom-call | tf_op jit(solution)/shard_map/pallas_call | solution.py:321
  30.1 0.6 %copy.8 = f32[8,256]{1,0:T(8,128)} copy(f32[8,256]{1,0:T(8,128)S(1)} %shard_map.64) | data formatting | bytes 16384

commit v4 on v3

--- a/solution.py
+++ b/solution.py
@@ -284,23 +284,23 @@
     rad_in.wait()
     w_in.wait()
     radial = rad_ref[...]
-    turned = jnp.dot(received_b, radial, preferred_element_type=F32)
-    product = radial.astype(F32) * turned
-    partial = product.reshape(A_DEV, LM, product.shape[1]).sum(axis=1) * w_ref[0]
-    chunk = product.shape[1] // n_energy
-    for e in range(n_energy):
-        p_send[e] = partial[:, e * chunk:(e + 1) * chunk]
+    chunk = radial.shape[1] // n_energy
 
     def p_copy(by):
         return pltpu.make_async_remote_copy(
-            src_ref=p_send.at[energy_at(by)], dst_ref=p_land.at[by - 1],
+            src_ref=p_send.at[by], dst_ref=p_land.at[by - 1],
             send_sem=p_send_sem.at[by - 1], recv_sem=p_recv_sem.at[by - 1],
             device_id={"energy": energy_at(by)}, device_id_type=MESH,
         )
 
-    for by in range(1, n_energy):
-        p_copy(by).start()
-    density = p_send[mine]
+    for by in sorted(range(n_energy), key=lambda d: -min(d, n_energy - d)):
+        part = rad_ref[:, pl.ds(pl.multiple_of(energy_at(by) * chunk, chunk), chunk)]
+        turned = jnp.dot(received_b, part, preferred_element_type=F32)
+        product = part.astype(F32) * turned
+        p_send[by] = product.reshape(A_DEV, LM, chunk).sum(axis=1) * w_ref[0]
+        if by:
+            p_copy(by).start()
+    density = p_send[0]
     for by in range(1, n_energy):
         p_copy(by).wait_recv()
         density = density + p_land[by - 1]

time: 30.8 us -> 30.8 us (level)
  no operation moved by 1% of the time
where the time goes in v4:
time: 30.8 us; the launch traced here: 30.7 us
  Pallas kernels  29.4 us (95%)
  between operations  0.66 us (2%)
  local copies, waits for them, and re-layouts  0.6 us (2%)
    pallas_call x1, Pallas kernels, shards(): pl.pallas_call(functools.partial(kernel, n_atom, n_energy), out_shape=plt...  29.4 us

profile of v4, /device:TPU:1, one launch (start us, length us, event | category | flops | bytes accessed | tf_op | source)
XLA Modules:
  0.0 30.7 jit_solution(17932527696877964040)
XLA Ops:
  0.7 29.4 %shard_map.64 = f32[8,256]{1,0:T(8,128)S(1)} custom-call(f32[128,16]{1,0:T(8,128)} %bitcast.5, bf16[128,1024]{1,0:T(8,128)(2,1)} %bitcast.4, f32[1]{0:T(128)S(6)} %copy.9.w_hbm, s32[8,64]{1,0:T(8,128)} %nbr_hbm.1, s32[8,64]{1,0:T(8,128)} %live_hbm.1, bf16[8,1024,1024]{2,1,0:T(8,128)(2,1)} %bitcast.3), custom_call_target="tpu_custom_call" | custom-call | tf_op jit(solution)/shard_map/pallas_call | solution.py:321
  30.1 0.6 %copy.8 = f32[8,256]{1,0:T(8,128)} copy(f32[8,256]{1,0:T(8,128)S(1)} %shard_map.64) | data formatting | bytes 16384
